TPU v7x, 32 devices: a whole 2x2x4 slice. The times are simulated.
32 devices in a mesh: leaf: 8 (over y, x, core), rhs: 4 (over z).
Axes of the slice: x: 2, y: 2, z: 4, core: 2. Of those that a mesh axis runs over, the one named last changes fastest.
Arguments:
- charges: bfloat16 [65536, 2048], P(('leaf', 'rhs')), may hold values from -6 to 6
- leaf_coef: bfloat16 [128, 256, 512], P(('leaf', 'rhs')), may hold values from -0.25 to 0.25
- leaf_rows: int32 [128, 256], P(('leaf', 'rhs')), may hold values from 0 to 511, as said below
- local_interp: bfloat16 [120, 256, 512], P('leaf'), may hold values from -0.25 to 0.25
- top_interp: bfloat16 [1792, 512], P('leaf'), may hold values from -0.25 to 0.25
Outputs:
- subtree_skel: bfloat16 [2048, 2048], P('leaf', 'rhs')
- top_skel: bfloat16 [1792, 2048], P('leaf', 'rhs')
Inputs may be any that keep to these rules, and one draw needn't show every extreme that they name: `leaf_rows`: each row holds 256 distinct positions.
All inputs are finite; a program needn't handle non-finite values.
Results may differ from a plain program's by a relative error of at most 0.012.
Values may be sent and summed in bfloat16 or wider, within the bound.
A program may use at most 64 MiB of HBM per device.

v0:
```python
import functools

import jax
import jax.numpy as jnp
from jax import lax
from jax.experimental import pallas as pl
from jax.experimental.pallas import tpu as pltpu
from jax.sharding import PartitionSpec as P

PARTS = 2


def bit(value, k):
    return (value // (1 << k)) % 2


def flip(value, offset, bits):
    out = 0
    for k in range(bits):
        a, b = bit(value, k), bit(offset, k)
        out = out + (a + b - 2 * a * b) * (1 << k)
    return out


def dot(a, b):
    return jnp.dot(a, b, preferred_element_type=jnp.float32)


def kernel(plan, charges, coef, rows, interp, top, root_out, top_out, *scratch):
    (points, mats, picks, nodes, tops, mixed, first, arrived, merged,
     tables, pairs, leaving, coming, padded, load_sem, send_sem, recv_sem,
     table_send, table_recv, pair_send, pair_recv, part_send, part_recv) = scratch
    pack = top.shape[0]
    R, L, H, cw = plan["R"], plan["L"], plan["H"], plan["cw"]
    leaves, S, M = plan["leaves"], plan["S"], plan["M"]
    m, n_leaf, early = plan["m"], plan["n_leaf"], plan["early"]
    total = leaves * R
    z = lax.axis_index("rhs")
    p = lax.axis_index("leaf")

    barrier = pltpu.get_barrier_semaphore()
    for b in range(m):
        pl.semaphore_signal(barrier, inc=1, device_id={"rhs": flip(z, 1 << b, m)},
                            device_id_type=pl.DeviceIdType.MESH)
    for delta in range(1, n_leaf):
        pl.semaphore_signal(barrier, inc=1, device_id={"leaf": flip(p, delta, L)},
                            device_id_type=pl.DeviceIdType.MESH)

    chunks = R * H
    order = sorted(
        [(b, d, h) for d in range(1, R) for h in range(H) for b in [(d & -d).bit_length() - 1]],
        key=lambda s: (-bin(s[1]).count("1"), s[2], s[0]))
    places = [(d, h) for _, d, h in order] + [(0, h) for h in range(H)]
    fetches = [1] * (L > 0) + list(range(2, n_leaf, 2))

    def table_copy(delta):
        part = pl.ds(0, S // 2) if delta == 1 else pl.ds(S // 2, pack - S // 2)
        k = fetches.index(delta)
        return pltpu.make_async_remote_copy(
            src_ref=top.at[part], dst_ref=tables.at[k, part], send_sem=table_send.at[k],
            recv_sem=table_recv.at[k], device_id={"leaf": flip(p, delta, L)},
            device_id_type=pl.DeviceIdType.MESH)


    def chunk_copy(i):
        d, h = places[i]
        column = (flip(z, d, m) * H + h) * cw
        return pltpu.make_async_copy(
            charges.at[:, pl.ds(pl.multiple_of(column, cw), cw)], points.at[i], load_sem.at[i])

    small = [(rows, picks)] + [(coef.at[n], mats.at[n, pl.ds(0, S)]) for n in range(leaves)]
    where = {}
    late = []
    for level in range(1, early + m + 1):
        count = max(leaves >> level, 1)
        if level <= early:
            start = total - (total >> level - 1) + z * count
        else:
            start = total - (total >> level - 1) + z // (1 << level - early)
        for k in range(count):
            where[level, k] = len(where)
            late.append((interp.at[start + k], nodes.at[where[level, k]]))
    late.append((top, tops))
    loads = [pltpu.make_async_copy(a, b, load_sem.at[chunks + i])
             for i, (a, b) in enumerate(small + late)]
    for copy in loads[:len(small)]:
        copy.start()
    chunk_copy(0).start()
    soon = len(small) + leaves - 1
    for copy in loads[len(small):soon]:
        copy.start()

    loads[0].wait()
    lanes = lax.broadcasted_iota(jnp.int32, (S, 128), 1)
    for n in range(leaves):
        across = jnp.transpose(jnp.broadcast_to(picks[n:n + 1, :], (128, S)))
        for t in range(M // 128):
            mats[n, S:, t * 128:(t + 1) * 128] = jnp.where(
                across == lanes + t * 128, 1.0, 0.0).astype(jnp.bfloat16)
    for i in range(1, chunks):
        chunk_copy(i).start()
    for copy in loads[soon:]:
        copy.start()
    pl.semaphore_wait(barrier, m + n_leaf - 1)
    for delta in fetches:
        table_copy(delta).start()
    for copy in loads[1:soon]:
        copy.wait()

    slot = {s: i for i, s in enumerate(order)}

    def first_of(d, h):
        return places.index((d, h))

    merge_keys = [(b, d, h) for b in range(1, m) for d in range(0, R, 1 << b) for h in range(H)]
    merge_at = {k: i for i, k in enumerate(merge_keys)}

    def held(b, d, h):
        return first.at[first_of(d, h)] if b == 0 else merged.at[merge_at[b, d, h]]

    def send(b, d, h):
        s = slot[b, d, h]
        return pltpu.make_async_remote_copy(
            src_ref=held(b, d, h), dst_ref=arrived.at[s], send_sem=send_sem.at[s],
            recv_sem=recv_sem.at[s], device_id={"rhs": flip(z, 1 << b, m)},
            device_id_type=pl.DeviceIdType.MESH)

    def chunk(i):
        chunk_copy(i).wait()
        for n in range(leaves):
            both = dot(mats[n], points[i, n * M:(n + 1) * M, :])
            mixed[n * S:(n + 1) * S, :] = (both[:S] + both[S:]).astype(jnp.bfloat16)
        for level in range(1, early + 1):
            for k in range(leaves >> level):
                node = dot(nodes[where[level, k]], mixed[2 * k * S:(2 * k + 2) * S, :])
                mixed[k * S:(k + 1) * S, :] = node.astype(jnp.bfloat16)
        first[i] = mixed[:S, :]

    def merge(b, d, h):
        s = slot[b, d + (1 << b), h]
        send(b, d + (1 << b), h).wait_recv()
        matrix = where[early + b + 1, 0]
        own = bit(z, b)
        mine = nodes[matrix, :, pl.ds(pl.multiple_of(own * S, S), S)]
        other = nodes[matrix, :, pl.ds(pl.multiple_of((1 - own) * S, S), S)]
        return (dot(mine, held(b, d, h)[...]) + dot(other, arrived[s])).astype(jnp.bfloat16)

    done = set()

    def ready(b, d, h):
        if b == 0 or (b, d, h) in done:
            return
        ready(b - 1, d, h)
        merged[merge_at[b, d, h]] = merge(b - 1, d, h)
        done.add((b, d, h))

    for i, (b, d, h) in enumerate(order):
        chunk(i)
        if b and not done:
            for copy in loads[soon:-1]:
                copy.wait()
        ready(b, d, h)
        send(b, d, h).start()
    for i in range(len(order), chunks):
        chunk(i)
    if m < 2:
        for copy in loads[soon:-1]:
            copy.wait()

    def pair_copy(level, h):
        height = S >> level - 1
        mine = pairs.at[level - 1, h, pl.ds(pl.multiple_of(p % 2 * height, height), height)]
        return pltpu.make_async_remote_copy(
            src_ref=mine, dst_ref=mine, send_sem=pair_send.at[level - 1, h],
            recv_sem=pair_recv.at[level - 1, h], device_id={"leaf": flip(p, 1, L)},
            device_id_type=pl.DeviceIdType.MESH)

    def part_copy(level, delta, h):
        i = delta // 2
        height = S >> level
        return pltpu.make_async_remote_copy(
            src_ref=leaving.at[level - 1, i, h, pl.ds(0, height)],
            dst_ref=coming.at[level - 1, i, h, pl.ds(0, height)],
            send_sem=part_send.at[level - 1, i, h], recv_sem=part_recv.at[level - 1, i, h],
            device_id={"leaf": flip(p, delta, L)}, device_id_type=pl.DeviceIdType.MESH)

    def put(level, h, value):
        height = S >> level - 1
        pairs[level - 1, h, pl.ds(pl.multiple_of(p % 2 * height, height), height), :] = value
        pair_copy(level, h).start()

    def begin(h):
        ready(m - 1, 0, h)
        root = merge(m - 1, 0, h) if m else held(0, 0, h)[...]
        root_out[:, h * cw:(h + 1) * cw] = root
        if L:
            put(1, h, root)

    def share(level, matrix, h):
        width = 2 * (S >> level - 1)
        chip = p % (1 << level) // 2
        rows = slice(S - (S >> level - 1), S - (S >> level))
        if width % 128 == 0:
            columns = pl.ds(pl.multiple_of(chip * width, width), width)
            return dot(matrix[rows, columns], pairs[level - 1, h, :width, :])
        padded[...] = jnp.zeros_like(padded)
        padded[pl.ds(pl.multiple_of(chip * width, width), width), :] = pairs[level - 1, h, :width, :]
        return dot(matrix[rows, :], padded[...])

    def climb(level, h):
        offset, count = S - (S >> level - 1), S >> level
        if level != 2:
            pair_copy(level, h).wait_recv()
        if level > 1:
            for delta in range(2, 1 << level, 2):
                leaving[level - 1, delta // 2, h, :count, :] = share(
                    level, tables.at[fetches.index(delta)], h).astype(jnp.bfloat16)
                part_copy(level, delta, h).start()
        value = share(level, tops, h)
        if level == 1 and L > 1:
            other = share(1, tables.at[0], h)
            pairs[1, h, pl.ds(pl.multiple_of((1 - p % 2) * count, count), count), :] = other.astype(jnp.bfloat16)
            pairs[1, h, pl.ds(pl.multiple_of(p % 2 * count, count), count), :] = value.astype(jnp.bfloat16)
        return value

    def finish(level, h, value):
        offset, count = S - (S >> level - 1), S >> level
        for delta in range(2, 1 << level, 2):
            part_copy(level, delta, h).wait_recv()
            value = value + coming[level - 1, delta // 2, h, :count, :].astype(jnp.float32)
        value = value.astype(jnp.bfloat16)
        if 2 <= level < L:
            put(level + 1, h, value)
        top_out[offset:offset + count, h * cw:(h + 1) * cw] = value

    for h in range(H):
        begin(h)
    loads[-1].wait()
    for level in range(1, L + 1):
        if level == 1:
            table_copy(1).wait_recv()
        if level == 2:
            for delta in fetches[1:]:
                table_copy(delta).wait_recv()
        values = [climb(level, h) for h in range(H)]
        for h in range(H):
            finish(level, h, values[h])

    for s in order:
        send(*s).wait_send()
    for delta in fetches:
        table_copy(delta).wait_send()
    for level in range(1, L + 1):
        for h in range(H):
            if level != 2:
                pair_copy(level, h).wait_send()
            for delta in range(2, 1 << level, 2):
                part_copy(level, delta, h).wait_send()


def store(root, top, root_out, top_out, sems):
    copies = [pltpu.make_async_copy(root, root_out, sems.at[0]),
              pltpu.make_async_copy(top, top_out, sems.at[1])]
    for copy in copies:
        copy.start()
    for copy in copies:
        copy.wait()


def local(charges, leaf_coef, leaf_rows, local_interp, top_interp):
    R, n_leaf = lax.axis_size("rhs"), lax.axis_size("leaf")
    leaves, S, M = leaf_coef.shape
    cols = charges.shape[1]
    m, L = R.bit_length() - 1, n_leaf.bit_length() - 1
    early = leaves.bit_length() - 1
    H = PARTS
    cw = cols // R // H
    plan = dict(R=R, L=L, H=H, cw=cw, leaves=leaves, S=S, M=M, m=m, n_leaf=n_leaf, early=early)
    node_count = leaves - 1 + m
    merge_count = max(sum(R >> b for b in range(1, m)) * H, 1)
    sends = max((R - 1) * H, 1)
    top_levels, chips = max(L, 1), max(n_leaf // 2, 1)
    bf = jnp.bfloat16
    pack = top_interp.shape[0]
    any_spec = pl.BlockSpec(memory_space=pl.ANY)
    vmem = pl.BlockSpec(memory_space=pltpu.VMEM)
    results = pl.pallas_call(
        functools.partial(kernel, plan),
        out_shape=(jax.ShapeDtypeStruct((S, cw * H), bf), jax.ShapeDtypeStruct((pack, cw * H), bf)),
        in_specs=[any_spec] * 5,
        out_specs=(vmem, vmem),
        scratch_shapes=[
            pltpu.VMEM((R * H, leaves * M, cw), bf),
            pltpu.VMEM((leaves, 2 * S, M), bf),
            pltpu.VMEM((leaves, S), jnp.int32),
            pltpu.VMEM((node_count, S, 2 * S), bf),
            pltpu.VMEM((pack, 2 * S), bf),
            pltpu.VMEM((leaves * S, cw), bf),
            pltpu.VMEM((R * H, S, cw), bf),
            pltpu.VMEM((sends, S, cw), bf),
            pltpu.VMEM((merge_count, S, cw), bf),
            pltpu.VMEM((max(n_leaf // 2, 1), pack, 2 * S), bf),
            pltpu.VMEM((top_levels, H, 2 * S, cw), bf),
            pltpu.VMEM((top_levels, chips, H, S // 4, cw), bf),
            pltpu.VMEM((top_levels, chips, H, S // 4, cw), bf),
            pltpu.VMEM((2 * S, cw), bf),
            pltpu.SemaphoreType.DMA((R * H + 2 + leaves + node_count,)),
            pltpu.SemaphoreType.DMA((sends,)),
            pltpu.SemaphoreType.DMA((sends,)),
            pltpu.SemaphoreType.DMA((max(n_leaf // 2, 1),)),
            pltpu.SemaphoreType.DMA((max(n_leaf // 2, 1),)),
            pltpu.SemaphoreType.DMA((top_levels, H)),
            pltpu.SemaphoreType.DMA((top_levels, H)),
            pltpu.SemaphoreType.DMA((top_levels, chips, H)),
            pltpu.SemaphoreType.DMA((top_levels, chips, H)),
        ],
        compiler_params=pltpu.CompilerParams(collective_id=0, has_side_effects=True,
                                             vmem_limit_bytes=60 * 1024 * 1024),
    )(charges, leaf_coef, leaf_rows, local_interp, top_interp)
    return pl.pallas_call(
        store,
        out_shape=(jax.ShapeDtypeStruct((S, cw * H), bf), jax.ShapeDtypeStruct((pack, cw * H), bf)),
        in_specs=[vmem, vmem],
        out_specs=(any_spec, any_spec),
        scratch_shapes=[pltpu.SemaphoreType.DMA((2,))],
    )(*results)


def solution(mesh):
    placed = (
        P(("leaf", "rhs"), None),
        P(("leaf", "rhs"), None, None),
        P(("leaf", "rhs"), None),
        P("leaf", None, None),
        P("leaf", None),
    )
    return jax.shard_map(
        local,
        mesh=mesh,
        in_specs=placed,
        out_specs=(P("leaf", "rhs"), P("leaf", "rhs")),
        check_vma=False,
    )
```

profile of v0, /device:TPU:0, one launch (start us, length us, event | category | flops | bytes accessed | tf_op | source)
XLA Modules:
  0.0 38.6 jit_solution(14366360677707495487)
XLA Ops:
  0.6 36.1 %shard_map.68 = (bf16[256,512]{1,0:T(8,128)(2,1)}, bf16[224,512]{1,0:T(8,128)(2,1)}) custom-call(bf16[2048,2048]{1,0:T(8,128)(2,1)} %charges.1, bf16[4,256,512]{2,1,0:T(8,128)(2,1)} %coef.1, s32[4,256]{1,0:T(4,128)} %rows.1, bf16[15,256,512]{2,1,0:T(8,128)(2,1)} %interp.1, bf16[224,512]{1,0:T(8,128)(2,1)} %top.1), custom_call_target="tpu_custom_call" | custom-call | tf_op jit(solution)/shard_map/pallas_call | solution.py:287
  36.8 1.8 %shard_map.69 = (bf16[256,512]{1,0:T(8,128)(2,1)}, bf16[224,512]{1,0:T(8,128)(2,1)}) custom-call(bf16[256,512]{1,0:T(8,128)(2,1)} %get-tuple-element.4.root, bf16[224,512]{1,0:T(8,128)(2,1)} %get-tuple-element.5.top), custom_call_target="tpu_custom_call" | custom-call | tf_op jit(solution)/shard_map/pallas_call | solution.py:320
where the time goes:
time: 38.8 us; the launch traced here: 38.6 us
  Pallas kernels  37.9 us (98%)
  between operations  0.64 us (2%)
    pallas_call x1, Pallas kernels, local(): pl.pallas_call(functools.partial(kernel, plan), out_shape=(jax.ShapeDtype...  36.1 us
    pallas_call x1, Pallas kernels, local(): pl.pallas_call(store, out_shape=(jax.ShapeDtypeStruct((S, cw * H), bf), j...  1.81 us

commit v1 on v0

v1 whole, which is shorter than its diff:
```python
import functools

import jax
import jax.numpy as jnp
from jax import lax
from jax.experimental import pallas as pl
from jax.experimental.pallas import tpu as pltpu
from jax.sharding import PartitionSpec as P

PIECE = 128
CHUNK = 256
LAG = 2
AHEAD = 5
MESH = pl.DeviceIdType.MESH


def bit(value, k):
    return (value // (1 << k)) % 2


def flip(value, offset, bits):
    out = 0
    for k in range(bits):
        a, b = bit(value, k), bit(offset, k)
        out = out + (a + b - 2 * a * b) * (1 << k)
    return out


def chosen(z, table):
    size = len(table)
    if len(set(table)) == 1:
        return table[0]
    out = 0
    for k, value in enumerate(table):
        differs = ((z - k + size) % size + size - 1) // size
        out = out + (1 - differs) * value
    return out


def dot(a, b):
    return jnp.dot(a, b, preferred_element_type=jnp.float32)


def up_block(R, i):
    return R - 1 - i


def block_order(R, Q, z):
    when = {}
    for c in range(R):
        if c > z:
            when[c] = LAG * z + (R - 1 - c) * Q
        elif c < z:
            when[c] = LAG * (R - 1 - z) + c * Q
        else:
            when[c] = final_step(R, Q, z)
    first = (lambda c: -c) if z < R / 2 else (lambda c: c)
    return sorted(range(R), key=lambda c: (c == z, when[c], first(c)))


def final_step(R, Q, z):
    below = LAG * z + (R - 1 - z) * Q if z > 0 else 0
    above = LAG * (R - 1 - z) + z * Q if z < R - 1 else 0
    return max(below, above)


def segments(S, L, n_leaf):
    out, start = [], 0
    for delta in range(n_leaf):
        first = max(delta.bit_length(), 1)
        rows = (S >> first - 1) - (S >> L)
        padded = -(-rows // 32) * 32
        out.append((start, first, rows, padded))
        start += padded
    return out, start


def kernel(plan, charges, coef, rows, interp, top, root_out, top_out, *scratch):
    (points, mats, picks, nodes, halves, ops, skel, leafw, tops, tables, wide, level_ops, parts,
     below, above, leaving, coming, load_sem, up_send, up_recv, down_send, down_recv,
     table_send, table_recv, part_send, part_recv) = scratch
    R, L, H, Q = plan["R"], plan["L"], plan["H"], plan["Q"]
    leaves, S, M = plan["leaves"], plan["S"], plan["M"]
    m, n_leaf, early = plan["m"], plan["n_leaf"], plan["early"]
    pack = top.shape[0]
    total = leaves * R
    bf = jnp.bfloat16
    z = lax.axis_index("rhs")
    p = lax.axis_index("leaf")
    segs, height = segments(S, L, n_leaf)
    orders = [block_order(R, Q, k) for k in range(R)]
    chunks = R * H

    barrier = pltpu.get_barrier_semaphore()
    if R > 1:
        @pl.when(z > 0)
        def _():
            pl.semaphore_signal(barrier, inc=1, device_id={"rhs": z - 1}, device_id_type=MESH)

        @pl.when(z < R - 1)
        def _():
            pl.semaphore_signal(barrier, inc=1, device_id={"rhs": z + 1}, device_id_type=MESH)
    for delta in range(1, n_leaf):
        pl.semaphore_signal(barrier, inc=1, device_id={"leaf": flip(p, delta, L)}, device_id_type=MESH)
    neighbours = chosen(z, [(k > 0) + (k < R - 1) for k in range(R)])

    def block(i):
        return chosen(z, [orders[k][i] for k in range(R)])

    def chunk_copy(i):
        column = (block(i // H) * H + i % H) * CHUNK
        return pltpu.make_async_copy(
            charges.at[:, pl.ds(pl.multiple_of(column, CHUNK), CHUNK)], points.at[i], load_sem.at[i])

    copies = [(rows, picks)] + [(coef.at[n], mats.at[n]) for n in range(leaves)]
    lead = len(copies)
    for b in range(m):
        index = total - (total >> early + b) + z // (1 << b + 1)
        copies.append((interp.at[index, :, pl.ds(pl.multiple_of(bit(z, b) * S, S), S)], halves.at[b]))
    where = {}
    for level in range(early, 0, -1):
        count = leaves >> level
        for k in range(count):
            where[level, k] = len(where)
            copies.append((interp.at[total - (total >> level - 1) + z * count + k], nodes.at[where[level, k]]))
    soon = len(copies)
    copies.append((top, tops))
    loads = [pltpu.make_async_copy(a, b, load_sem.at[chunks + i]) for i, (a, b) in enumerate(copies)]

    for copy in loads[:lead]:
        copy.start()
    for copy in loads[lead:soon]:
        copy.start()
    chunk_copy(0).start()

    def table_copy(delta):
        start, first, count, _ = segs[delta]
        part = pl.ds(S - (S >> first - 1), pack - S + (S >> first - 1))
        return pltpu.make_async_remote_copy(
            src_ref=top.at[part], dst_ref=tables.at[delta - 1, part], send_sem=table_send.at[delta - 1],
            recv_sem=table_recv.at[delta - 1], device_id={"leaf": flip(p, delta, L)}, device_id_type=MESH)

    def send_up(i):
        return pltpu.make_async_remote_copy(
            src_ref=parts.at[i], dst_ref=below.at[i], send_sem=up_send.at[i], recv_sem=up_recv.at[i],
            device_id={"rhs": z + 1}, device_id_type=MESH)

    def send_down(i):
        return pltpu.make_async_remote_copy(
            src_ref=parts.at[i], dst_ref=above.at[i], send_sem=down_send.at[i], recv_sem=down_recv.at[i],
            device_id={"rhs": z - 1}, device_id_type=MESH)

    def part_copy(q, delta):
        start, _, _, padded = segs[delta]
        ref = pl.ds(start, padded)
        return pltpu.make_async_remote_copy(
            src_ref=leaving.at[q, ref], dst_ref=coming.at[q, ref], send_sem=part_send.at[q, delta - 1],
            recv_sem=part_recv.at[q, delta - 1], device_id={"leaf": flip(p, delta, L)}, device_id_type=MESH)

    @pl.when(z == 0)
    def _():
        for q in range(Q):
            below[q] = jnp.zeros((S, PIECE), bf)

    @pl.when(z == R - 1)
    def _():
        for q in range(Q):
            above[(R - 1) * Q + q] = jnp.zeros((S, PIECE), bf)

    for copy in loads[:lead]:
        copy.wait()
    lanes = lax.broadcasted_iota(jnp.int32, (S, 128), 1)
    for n in range(leaves):
        across = jnp.transpose(jnp.broadcast_to(picks[n:n + 1, :], (128, S)))
        for t in range(M // 128):
            part = slice(t * 128, (t + 1) * 128)
            mats[n, :, part] = (mats[n, :, part].astype(jnp.float32)
                                + jnp.where(across == lanes + t * 128, 1.0, 0.0)).astype(bf)
    for i in range(1, chunks):
        chunk_copy(i).start()
    loads[-1].start()
    pl.semaphore_wait(barrier, neighbours + n_leaf - 1)
    for delta in range(1, n_leaf):
        table_copy(delta).start()
    for copy in loads[lead:soon]:
        copy.wait()

    def leaf_stage(i):
        chunk_copy(i).wait()
        for n in range(leaves):
            leafw[n * S:(n + 1) * S, :] = dot(mats[n], points[i, n * M:(n + 1) * M, :]).astype(bf)

    def compose():
        op = None
        for b in range(m):
            if b == 0:
                op = halves[0]
            else:
                op = dot(halves[b], op).astype(bf)
        current = [op]
        for level in range(early, 0, -1):
            following = []
            for k in range(leaves >> level):
                matrix = nodes[where[level, k]]
                value = matrix if current[k] is None else dot(current[k], matrix).astype(bf)
                if level == 1:
                    skel[:, 2 * k * S:(2 * k + 2) * S] = value
                else:
                    ops[where[level, k]] = value
                    following += [ops[where[level, k], :, :S], ops[where[level, k], :, S:]]
            current = following
        if early == 0:
            rows_at = lax.broadcasted_iota(jnp.int32, (S, S), 0)
            same = jnp.where(rows_at == lax.broadcasted_iota(jnp.int32, (S, S), 1), 1.0, 0.0).astype(bf)
            skel[...] = same if op is None else op

    def chunk(i):
        leaf_stage(i)
        if i == 0:
            compose()
        value = dot(skel[...], leafw[...]).astype(bf)
        c = block(i // H)
        base = c * Q + i % H * (CHUNK // PIECE)
        for j in range(CHUNK // PIECE):
            parts[base + j] = value[:, j * PIECE:(j + 1) * PIECE]
        if i < chunks - H and R > 1:
            @pl.when(z == 0)
            def _():
                for j in range(CHUNK // PIECE):
                    send_up(base + j).start()

            @pl.when(z == R - 1)
            def _():
                for j in range(CHUNK // PIECE):
                    send_down(base + j).start()

    def prepare_top():
        loads[-1].wait()
        for delta in range(1, n_leaf):
            table_copy(delta).wait_recv()
        for level in range(1, L + 1):
            offset, count = S - (S >> level - 1), S >> level
            half = pl.ds(pl.multiple_of(bit(p, level - 1) * S, S), S)
            for delta in range(1 << level):
                source = tops if delta == 0 else tables.at[delta - 1]
                rows_of = source[offset:offset + count, half]
                if level == 1:
                    put_top(level, delta, rows_of)
                else:
                    level_ops[1, delta * count:(delta + 1) * count, :] = rows_of
            if level > 1:
                value = dot(level_ops[1], level_ops[0]).astype(bf)
                for delta in range(1 << level):
                    put_top(level, delta, value[delta * count:(delta + 1) * count])

    def put_top(level, delta, value):
        start, first, _, _ = segs[delta]
        offset, count = (S >> first - 1) - (S >> level - 1), S >> level
        wide[start + offset:start + offset + count, :] = value
        if level < L:
            place = flip(p, delta, L) % (1 << level)
            level_ops[0, pl.ds(pl.multiple_of(place * count, count), count), :] = value

    def add_into(i, other):
        parts[i] = (parts[i].astype(jnp.float32) + other[i].astype(jnp.float32)).astype(bf)

    def any_device(test):
        return any(test(k) for k in range(R))

    def step(t):
        if any_device(lambda k: k > 0 and 0 <= t - LAG * k < (R - 1 - k) * Q):
            s = t - LAG * z

            @pl.when((z > 0) & (s >= 0) & (s < (R - 1 - z) * Q))
            def _():
                i = (R - 1 - s // Q) * Q + s % Q
                send_up(i).wait_recv()
                add_into(i, below)
                send_up(i).start()

        if any_device(lambda k: k < R - 1 and 0 <= t - LAG * (R - 1 - k) < k * Q):
            s_down = t - LAG * (R - 1 - z)

            @pl.when((z < R - 1) & (s_down >= 0) & (s_down < z * Q))
            def _():
                send_down(s_down).wait_recv()
                add_into(s_down, above)
                send_down(s_down).start()

        finals = [final_step(R, Q, k) for k in range(R)]
        if any_device(lambda k: 0 <= t - finals[k] < Q):
            q = t - chosen(z, finals)

            @pl.when((q >= 0) & (q < Q))
            def _():
                finish(q)

    def finish(q):
        i = z * Q + q
        if R > 1:
            @pl.when(z > 0)
            def _():
                send_up(i).wait_recv()

            @pl.when(z < R - 1)
            def _():
                send_down(i).wait_recv()
        root = (parts[i].astype(jnp.float32) + below[i].astype(jnp.float32)
                + above[i].astype(jnp.float32)).astype(bf)
        root_out[:, pl.ds(pl.multiple_of(q * PIECE, PIECE), PIECE)] = root
        leaving[q] = dot(wide[...], root).astype(bf)
        for delta in range(1, n_leaf):
            part_copy(q, delta).start()

    steps = max(final_step(R, Q, k) for k in range(R)) + Q
    needed = []
    for t in range(steps):
        need = 0
        for k in range(R):
            s, s_down = t - LAG * k, t - LAG * (R - 1 - k)
            blocks = []
            if k > 0 and 0 <= s < (R - 1 - k) * Q:
                blocks.append((R - 1 - s // Q, s % Q))
            if k < R - 1 and 0 <= s_down < k * Q:
                blocks.append((s_down // Q, s_down % Q))
            if 0 <= t - final_step(R, Q, k) < Q:
                blocks.append((k, t - final_step(R, Q, k)))
            for c, q in blocks:
                need = max(need, orders[k].index(c) * H + q // (CHUNK // PIECE) + 1)
        needed.append(need)
    earliest = min(final_step(R, Q, k) for k in range(R))

    made = 0
    prepared = False
    for t in range(steps):
        while made < chunks and (made < needed[t] or made < min(t + AHEAD, chunks)):
            chunk(made)
            made += 1
        if made == chunks and not prepared or t == earliest and not prepared:
            prepare_top()
            prepared = True
        step(t)

    for q in range(Q):
        for delta in range(1, n_leaf):
            part_copy(q, delta).wait_recv()
        for level in range(1, L + 1):
            offset, count = S - (S >> level - 1), S >> level
            value = None
            for delta in range(1 << level):
                start, first, _, _ = segs[delta]
                at = start + (S >> first - 1) - (S >> level - 1)
                source = leaving if delta == 0 else coming
                term = source[q, at:at + count, :].astype(jnp.float32)
                value = term if value is None else value + term
            top_out[offset:offset + count, q * PIECE:(q + 1) * PIECE] = value.astype(bf)

    for delta in range(1, n_leaf):
        table_copy(delta).wait_send()
        for q in range(Q):
            part_copy(q, delta).wait_send()
    if R > 1:
        for i in range(R * Q):
            @pl.when((z < R - 1) & (z < i // Q))
            def _():
                send_up(i).wait_send()

            @pl.when((z > 0) & (z > i // Q))
            def _():
                send_down(i).wait_send()


def store(root, top, root_out, top_out, sems):
    copies = [pltpu.make_async_copy(root, root_out, sems.at[0]),
              pltpu.make_async_copy(top, top_out, sems.at[1])]
    for copy in copies:
        copy.start()
    for copy in copies:
        copy.wait()


def local(charges, leaf_coef, leaf_rows, local_interp, top_interp):
    R, n_leaf = lax.axis_size("rhs"), lax.axis_size("leaf")
    leaves, S, M = leaf_coef.shape
    cols = charges.shape[1]
    m, L = R.bit_length() - 1, n_leaf.bit_length() - 1
    early = leaves.bit_length() - 1
    width = cols // R
    H, Q = width // CHUNK, width // PIECE
    plan = dict(R=R, L=L, H=H, Q=Q, leaves=leaves, S=S, M=M, m=m, n_leaf=n_leaf, early=early)
    bf = jnp.bfloat16
    pack = top_interp.shape[0]
    _, height = segments(S, L, n_leaf)
    any_spec = pl.BlockSpec(memory_space=pl.ANY)
    vmem = pl.BlockSpec(memory_space=pltpu.VMEM)
    node_count = max(leaves - 1, 1)
    peers = max(n_leaf - 1, 1)
    dma = pltpu.SemaphoreType.DMA
    results = pl.pallas_call(
        functools.partial(kernel, plan),
        out_shape=(jax.ShapeDtypeStruct((S, width), bf), jax.ShapeDtypeStruct((pack, width), bf)),
        in_specs=[any_spec] * 5,
        out_specs=(vmem, vmem),
        scratch_shapes=[
            pltpu.VMEM((R * H, leaves * M, CHUNK), bf),
            pltpu.VMEM((leaves, S, M), bf),
            pltpu.VMEM((leaves, S), jnp.int32),
            pltpu.VMEM((node_count, S, 2 * S), bf),
            pltpu.VMEM((max(m, 1), S, S), bf),
            pltpu.VMEM((node_count, S, 2 * S), bf),
            pltpu.VMEM((S, leaves * S), bf),
            pltpu.VMEM((leaves * S, CHUNK), bf),
            pltpu.VMEM((pack, 2 * S), bf),
            pltpu.VMEM((peers, pack, 2 * S), bf),
            pltpu.VMEM((height, S), bf),
            pltpu.VMEM((2, S, S), bf),
            pltpu.VMEM((R * Q, S, PIECE), bf),
            pltpu.VMEM((R * Q, S, PIECE), bf),
            pltpu.VMEM((R * Q, S, PIECE), bf),
            pltpu.VMEM((Q, height, PIECE), bf),
            pltpu.VMEM((Q, height, PIECE), bf),
            dma((R * H + 2 + leaves + node_count + m,)),
            dma((R * Q,)),
            dma((R * Q,)),
            dma((R * Q,)),
            dma((R * Q,)),
            dma((peers,)),
            dma((peers,)),
            dma((Q, peers)),
            dma((Q, peers)),
        ],
        compiler_params=pltpu.CompilerParams(collective_id=0, has_side_effects=True,
                                             vmem_limit_bytes=60 * 1024 * 1024),
    )(charges, leaf_coef, leaf_rows, local_interp, top_interp)
    return pl.pallas_call(
        store,
        out_shape=(jax.ShapeDtypeStruct((S, width), bf), jax.ShapeDtypeStruct((pack, width), bf)),
        in_specs=[vmem, vmem],
        out_specs=(any_spec, any_spec),
        scratch_shapes=[pltpu.SemaphoreType.DMA((2,))],
    )(*results)


def solution(mesh):
    placed = (
        P(("leaf", "rhs"), None),
        P(("leaf", "rhs"), None, None),
        P(("leaf", "rhs"), None),
        P("leaf", None, None),
        P("leaf", None),
    )
    return jax.shard_map(
        local,
        mesh=mesh,
        in_specs=placed,
        out_specs=(P("leaf", "rhs"), P("leaf", "rhs")),
        check_vma=False,
    )
```

time: 38.8 us -> 32.9 us (0.85)
  the two profiles are of different devices: /device:TPU:0 before, /device:TPU:17 now
where the time goes in v1:
time: 32.9 us; the launch traced here: 32.3 us
  Pallas kernels  31.6 us (96%)
  between operations  0.64 us (2%)
    pallas_call x1, Pallas kernels, local(): pl.pallas_call(functools.partial(kernel, plan), out_shape=(jax.ShapeDtype...  29.8 us
    pallas_call x1, Pallas kernels, local(): pl.pallas_call(store, out_shape=(jax.ShapeDtypeStruct((S, width), bf), ja...  1.81 us

profile of v1, /device:TPU:17, one launch (start us, length us, event | category | flops | bytes accessed | tf_op | source)
XLA Modules:
  0.0 32.3 jit_solution(5818094827469088283)
XLA Ops:
  0.6 29.8 %shard_map.68 = (bf16[256,512]{1,0:T(8,128)(2,1)}, bf16[224,512]{1,0:T(8,128)(2,1)}) custom-call(bf16[2048,2048]{1,0:T(8,128)(2,1)} %charges.1, bf16[4,256,512]{2,1,0:T(8,128)(2,1)} %coef.1, s32[4,256]{1,0:T(4,128)} %rows.1, bf16[15,256,512]{2,1,0:T(8,128)(2,1)} %interp.1, bf16[224,512]{1,0:T(8,128)(2,1)} %top.1), custom_call_target="tpu_custom_call" | custom-call | tf_op jit(solution)/shard_map/pallas_call | solution.py:399
  30.5 1.8 %shard_map.69 = (bf16[256,512]{1,0:T(8,128)(2,1)}, bf16[224,512]{1,0:T(8,128)(2,1)}) custom-call(bf16[256,512]{1,0:T(8,128)(2,1)} %get-tuple-element.4.root, bf16[224,512]{1,0:T(8,128)(2,1)} %get-tuple-element.5.top), custom_call_target="tpu_custom_call" | custom-call | tf_op jit(solution)/shard_map/pallas_call | solution.py:435

commit v2 on v1

--- a/solution.py
+++ b/solution.py
@@ -11,6 +11,9 @@
 CHUNK = 256
 LAG = 2
 AHEAD = 5
+EARLY = 1
+TABLES = 2
+WAIT = 3
 MESH = pl.DeviceIdType.MESH
 
 
@@ -77,8 +80,8 @@
 
 def kernel(plan, charges, coef, rows, interp, top, root_out, top_out, *scratch):
     (points, mats, picks, nodes, halves, ops, skel, leafw, tops, tables, wide, level_ops, parts,
-     below, above, leaving, coming, load_sem, up_send, up_recv, down_send, down_recv,
-     table_send, table_recv, part_send, part_recv) = scratch
+     below, above, leaving, coming, sums, extra, load_sem, up_send, up_recv, down_send, down_recv,
+     table_send, table_recv, part_send, part_recv, sum_send, sum_recv) = scratch
     R, L, H, Q = plan["R"], plan["L"], plan["H"], plan["Q"]
     leaves, S, M = plan["leaves"], plan["S"], plan["M"]
     m, n_leaf, early = plan["m"], plan["n_leaf"], plan["early"]
@@ -90,6 +93,8 @@
     segs, height = segments(S, L, n_leaf)
     orders = [block_order(R, Q, k) for k in range(R)]
     chunks = R * H
+    hurried = EARLY if R > 1 else 0
+    earliest = min(final_step(R, Q, k) for k in range(R))
 
     barrier = pltpu.get_barrier_semaphore()
     if R > 1:
@@ -100,8 +105,8 @@
         @pl.when(z < R - 1)
         def _():
             pl.semaphore_signal(barrier, inc=1, device_id={"rhs": z + 1}, device_id_type=MESH)
-    for delta in range(1, n_leaf):
-        pl.semaphore_signal(barrier, inc=1, device_id={"leaf": flip(p, delta, L)}, device_id_type=MESH)
+    for b in range(L):
+        pl.semaphore_signal(barrier, inc=1, device_id={"leaf": flip(p, 1 << b, L)}, device_id_type=MESH)
     neighbours = chosen(z, [(k > 0) + (k < R - 1) for k in range(R)])
 
     def block(i):
@@ -123,8 +128,8 @@
         for k in range(count):
             where[level, k] = len(where)
             copies.append((interp.at[total - (total >> level - 1) + z * count + k], nodes.at[where[level, k]]))
+    copies.append((top, tops))
     soon = len(copies)
-    copies.append((top, tops))
     loads = [pltpu.make_async_copy(a, b, load_sem.at[chunks + i]) for i, (a, b) in enumerate(copies)]
 
     for copy in loads[:lead]:
@@ -133,12 +138,29 @@
         copy.start()
     chunk_copy(0).start()
 
-    def table_copy(delta):
-        start, first, count, _ = segs[delta]
-        part = pl.ds(S - (S >> first - 1), pack - S + (S >> first - 1))
-        return pltpu.make_async_remote_copy(
-            src_ref=top.at[part], dst_ref=tables.at[delta - 1, part], send_sem=table_send.at[delta - 1],
-            recv_sem=table_recv.at[delta - 1], device_id={"leaf": flip(p, delta, L)}, device_id_type=MESH)
+    def table_copies(delta):
+        peer = flip(p, delta, L)
+        out = []
+        for level in range(segs[delta][1], L + 1):
+            part = pl.ds(S - (S >> level - 1), S >> level)
+            half = pl.ds(pl.multiple_of(bit(peer, level - 1) * S, S), S)
+            out.append(pltpu.make_async_remote_copy(
+                src_ref=tops.at[part, half], dst_ref=tables.at[delta - 1, part],
+                send_sem=table_send.at[delta - 1, level - 1], recv_sem=table_recv.at[delta - 1, level - 1],
+                device_id={"leaf": peer}, device_id_type=MESH))
+        return out
+
+    stages = [[d for d in range(1, n_leaf) if bin(d).count("1") == k] for k in range(L + 1)]
+
+    def table_stage(k):
+        if k > 1:
+            for delta in stages[k - 1]:
+                for copy in table_copies(delta):
+                    copy.wait_recv()
+        if k <= L:
+            for delta in stages[k]:
+                for copy in table_copies(delta):
+                    copy.start()
 
     def send_up(i):
         return pltpu.make_async_remote_copy(
@@ -156,6 +178,11 @@
         return pltpu.make_async_remote_copy(
             src_ref=leaving.at[q, ref], dst_ref=coming.at[q, ref], send_sem=part_send.at[q, delta - 1],
             recv_sem=part_recv.at[q, delta - 1], device_id={"leaf": flip(p, delta, L)}, device_id_type=MESH)
+
+    if hurried:
+        @pl.when(chosen(z, [int(k in (1, R - 2)) for k in range(R)]) == 0)
+        def _():
+            extra[...] = jnp.zeros_like(extra)
 
     @pl.when(z == 0)
     def _():
@@ -178,10 +205,6 @@
                                 + jnp.where(across == lanes + t * 128, 1.0, 0.0)).astype(bf)
     for i in range(1, chunks):
         chunk_copy(i).start()
-    loads[-1].start()
-    pl.semaphore_wait(barrier, neighbours + n_leaf - 1)
-    for delta in range(1, n_leaf):
-        table_copy(delta).start()
     for copy in loads[lead:soon]:
         copy.wait()
 
@@ -223,6 +246,9 @@
         base = c * Q + i % H * (CHUNK // PIECE)
         for j in range(CHUNK // PIECE):
             parts[base + j] = value[:, j * PIECE:(j + 1) * PIECE]
+        if i == 0:
+            pl.semaphore_wait(barrier, neighbours + L)
+            table_stage(1)
         if i < chunks - H and R > 1:
             @pl.when(z == 0)
             def _():
@@ -235,15 +261,14 @@
                     send_down(base + j).start()
 
     def prepare_top():
-        loads[-1].wait()
-        for delta in range(1, n_leaf):
-            table_copy(delta).wait_recv()
         for level in range(1, L + 1):
             offset, count = S - (S >> level - 1), S >> level
             half = pl.ds(pl.multiple_of(bit(p, level - 1) * S, S), S)
             for delta in range(1 << level):
-                source = tops if delta == 0 else tables.at[delta - 1]
-                rows_of = source[offset:offset + count, half]
+                if delta == 0:
+                    rows_of = tops[offset:offset + count, half]
+                else:
+                    rows_of = tables[delta - 1, offset:offset + count, :]
                 if level == 1:
                     put_top(level, delta, rows_of)
                 else:
@@ -287,11 +312,21 @@
                 add_into(s_down, above)
                 send_down(s_down).start()
 
+        for j in range(hurried):
+            q = Q - hurried + j
+            if any_device(lambda k: late(k) and t == hurry_step(k, q)):
+                now = chosen(z, [late(k) * (t == hurry_step(k, q)) for k in range(R)])
+
+                @pl.when(now == 1)
+                def _():
+                    hurry(q)
+
         finals = [final_step(R, Q, k) for k in range(R)]
         if any_device(lambda k: 0 <= t - finals[k] < Q):
             q = t - chosen(z, finals)
-
-            @pl.when((q >= 0) & (q < Q))
+            last = chosen(z, [Q - hurried * late(k) for k in range(R)])
+
+            @pl.when((q >= 0) & (q < last))
             def _():
                 finish(q)
 
@@ -308,9 +343,81 @@
         root = (parts[i].astype(jnp.float32) + below[i].astype(jnp.float32)
                 + above[i].astype(jnp.float32)).astype(bf)
         root_out[:, pl.ds(pl.multiple_of(q * PIECE, PIECE), PIECE)] = root
-        leaving[q] = dot(wide[...], root).astype(bf)
+        spread(q, root)
+
+    def spread(q, value):
+        leaving[q] = dot(wide[...], value).astype(bf)
         for delta in range(1, n_leaf):
             part_copy(q, delta).start()
+
+    def late(k):
+        return int(R > 1 and k in (1, R - 2))
+
+    def hurry_step(k, q):
+        other = LAG * (R - 1 - k) + k * Q if k == 1 else LAG * k + (R - 1 - k) * Q
+        return max((other if R > 2 else 0) + q, earliest)
+
+    def hurry(q):
+        i = z * Q + q
+
+        @pl.when(z == 1)
+        def _():
+            if R > 2:
+                send_down(i).wait_recv()
+            add_into(i, above)
+
+        @pl.when(z == R - 2)
+        def _():
+            if R > 2:
+                send_up(i).wait_recv()
+            add_into(i, below)
+
+        spread(q, parts[i])
+
+    def sum_copy(j, upward):
+        return pltpu.make_async_remote_copy(
+            src_ref=sums.at[j], dst_ref=extra.at[j], send_sem=sum_send.at[j], recv_sem=sum_recv.at[j],
+            device_id={"rhs": z + 1 if upward else z - 1}, device_id_type=MESH)
+
+    def gather(q):
+        for delta in range(1, n_leaf):
+            part_copy(q, delta).wait_recv()
+        out = []
+        for level in range(1, L + 1):
+            offset, count = S - (S >> level - 1), S >> level
+            value = None
+            for delta in range(1 << level):
+                start, first, _, _ = segs[delta]
+                at = start + (S >> first - 1) - (S >> level - 1)
+                source = leaving if delta == 0 else coming
+                term = source[q, at:at + count, :].astype(jnp.float32)
+                value = term if value is None else value + term
+            out.append((offset, count, value))
+        return out
+
+    def end_begin():
+        @pl.when((z == 0) | (z == R - 1))
+        def _():
+            target = chosen(z, [1 if k == 0 else R - 2 for k in range(R)])
+            for j in range(hurried):
+                spread(Q + j, parts[target * Q + Q - hurried + j])
+
+    def end_finish():
+        @pl.when((z == 0) | (z == R - 1))
+        def _():
+            for j in range(hurried):
+                for offset, count, value in gather(Q + j):
+                    sums[j, offset:offset + count, :] = value.astype(bf)
+
+        @pl.when(z == 0)
+        def _():
+            for j in range(hurried):
+                sum_copy(j, True).start()
+
+        @pl.when(z == R - 1)
+        def _():
+            for j in range(hurried):
+                sum_copy(j, False).start()
 
     steps = max(final_step(R, Q, k) for k in range(R)) + Q
     needed = []
@@ -327,38 +434,81 @@
                 blocks.append((k, t - final_step(R, Q, k)))
             for c, q in blocks:
                 need = max(need, orders[k].index(c) * H + q // (CHUNK // PIECE) + 1)
+        for j in range(hurried):
+            q = Q - hurried + j
+            for k in range(R):
+                if late(k) and t == hurry_step(k, q):
+                    need = max(need, orders[k].index(k) * H + q // (CHUNK // PIECE) + 1)
+        if t >= earliest:
+            need = max(need, chunks if hurried else 0)
         needed.append(need)
-    earliest = min(final_step(R, Q, k) for k in range(R))
-
-    made = 0
-    prepared = False
+
+    made, stage = 0, 2
     for t in range(steps):
         while made < chunks and (made < needed[t] or made < min(t + AHEAD, chunks)):
             chunk(made)
             made += 1
-        if made == chunks and not prepared or t == earliest and not prepared:
+            if made == AHEAD and stage == 2:
+                table_stage(stage)
+                stage += 1
+        if made == chunks and stage <= L and t < earliest and t >= TABLES * (stage - 1):
+            table_stage(stage)
+            stage += 1
+        if t == earliest:
+            while stage <= L + 1:
+                table_stage(stage)
+                stage += 1
             prepare_top()
-            prepared = True
+            if hurried:
+                end_begin()
+        if hurried and t == earliest + WAIT:
+            end_finish()
         step(t)
 
     for q in range(Q):
-        for delta in range(1, n_leaf):
-            part_copy(q, delta).wait_recv()
-        for level in range(1, L + 1):
-            offset, count = S - (S >> level - 1), S >> level
-            value = None
-            for delta in range(1 << level):
-                start, first, _, _ = segs[delta]
-                at = start + (S >> first - 1) - (S >> level - 1)
-                source = leaving if delta == 0 else coming
-                term = source[q, at:at + count, :].astype(jnp.float32)
-                value = term if value is None else value + term
-            top_out[offset:offset + count, q * PIECE:(q + 1) * PIECE] = value.astype(bf)
+        j = q - (Q - hurried)
+        columns = slice(q * PIECE, (q + 1) * PIECE)
+        values = gather(q)
+        if j >= 0:
+            i = z * Q + q
+
+            @pl.when(z == 1)
+            def _():
+                send_up(i).wait_recv()
+                root_out[:, columns] = (parts[i].astype(jnp.float32) + below[i].astype(jnp.float32)).astype(bf)
+                sum_copy(j, True).wait_recv()
+
+            @pl.when(z == R - 2)
+            def _():
+                send_down(i).wait_recv()
+                root_out[:, columns] = (parts[i].astype(jnp.float32) + above[i].astype(jnp.float32)).astype(bf)
+                sum_copy(j, False).wait_recv()
+        for offset, count, value in values:
+            if j >= 0:
+                value = value + extra[j, offset:offset + count, :].astype(jnp.float32)
+            top_out[offset:offset + count, columns] = value.astype(bf)
 
     for delta in range(1, n_leaf):
-        table_copy(delta).wait_send()
+        for copy in table_copies(delta):
+            copy.wait_send()
         for q in range(Q):
             part_copy(q, delta).wait_send()
+    if hurried:
+        @pl.when((z == 0) | (z == R - 1))
+        def _():
+            for j in range(hurried):
+                for delta in range(1, n_leaf):
+                    part_copy(Q + j, delta).wait_send()
+
+        @pl.when(z == 0)
+        def _():
+            for j in range(hurried):
+                sum_copy(j, True).wait_send()
+
+        @pl.when(z == R - 1)
+        def _():
+            for j in range(hurried):
+                sum_copy(j, False).wait_send()
     if R > 1:
         for i in range(R * Q):
             @pl.when((z < R - 1) & (z < i // Q))
@@ -411,23 +561,27 @@
             pltpu.VMEM((S, leaves * S), bf),
             pltpu.VMEM((leaves * S, CHUNK), bf),
             pltpu.VMEM((pack, 2 * S), bf),
-            pltpu.VMEM((peers, pack, 2 * S), bf),
+            pltpu.VMEM((peers, pack, S), bf),
             pltpu.VMEM((height, S), bf),
             pltpu.VMEM((2, S, S), bf),
             pltpu.VMEM((R * Q, S, PIECE), bf),
             pltpu.VMEM((R * Q, S, PIECE), bf),
             pltpu.VMEM((R * Q, S, PIECE), bf),
-            pltpu.VMEM((Q, height, PIECE), bf),
-            pltpu.VMEM((Q, height, PIECE), bf),
+            pltpu.VMEM((Q + EARLY, height, PIECE), bf),
+            pltpu.VMEM((Q + EARLY, height, PIECE), bf),
+            pltpu.VMEM((max(EARLY, 1), pack, PIECE), bf),
+            pltpu.VMEM((max(EARLY, 1), pack, PIECE), bf),
             dma((R * H + 2 + leaves + node_count + m,)),
             dma((R * Q,)),
             dma((R * Q,)),
             dma((R * Q,)),
             dma((R * Q,)),
-            dma((peers,)),
-            dma((peers,)),
-            dma((Q, peers)),
-            dma((Q, peers)),
+            dma((peers, max(L, 1))),
+            dma((peers, max(L, 1))),
+            dma((Q + EARLY, peers)),
+            dma((Q + EARLY, peers)),
+            dma((max(EARLY, 1),)),
+            dma((max(EARLY, 1),)),
         ],
         compiler_params=pltpu.CompilerParams(collective_id=0, has_side_effects=True,
                                              vmem_limit_bytes=60 * 1024 * 1024),

time: 32.9 us -> 35.1 us (1.067)
  the two profiles are of different devices: /device:TPU:17 before, /device:TPU:9 now
where the time goes in v2:
time: 35.1 us; the launch traced here: 34.9 us
  Pallas kernels  34.3 us (98%)
  between operations  0.64 us (2%)
    pallas_call x1, Pallas kernels, local(): pl.pallas_call(functools.partial(kernel, plan), out_shape=(jax.ShapeDtype...  32.5 us
    pallas_call x1, Pallas kernels, local(): pl.pallas_call(store, out_shape=(jax.ShapeDtypeStruct((S, width), bf), ja...  1.81 us

profile of v2, /device:TPU:9, one launch (start us, length us, event | category | flops | bytes accessed | tf_op | source)
XLA Modules:
  0.0 34.9 jit_solution(3779884244894697978)
XLA Ops:
  0.6 32.5 %shard_map.68 = (bf16[256,512]{1,0:T(8,128)(2,1)}, bf16[224,512]{1,0:T(8,128)(2,1)}) custom-call(bf16[2048,2048]{1,0:T(8,128)(2,1)} %charges.1, bf16[4,256,512]{2,1,0:T(8,128)(2,1)} %coef.1, s32[4,256]{1,0:T(4,128)} %rows.1, bf16[15,256,512]{2,1,0:T(8,128)(2,1)} %interp.1, bf16[224,512]{1,0:T(8,128)(2,1)} %top.1), custom_call_target="tpu_custom_call" | custom-call | tf_op jit(solution)/shard_map/pallas_call | solution.py:549
  33.1 1.8 %shard_map.69 = (bf16[256,512]{1,0:T(8,128)(2,1)}, bf16[224,512]{1,0:T(8,128)(2,1)}) custom-call(bf16[256,512]{1,0:T(8,128)(2,1)} %get-tuple-element.4.root, bf16[224,512]{1,0:T(8,128)(2,1)} %get-tuple-element.5.top), custom_call_target="tpu_custom_call" | custom-call | tf_op jit(solution)/shard_map/pallas_call | solution.py:589

commit v3 on v2

--- a/solution.py
+++ b/solution.py
@@ -11,7 +11,7 @@
 CHUNK = 256
 LAG = 2
 AHEAD = 5
-EARLY = 1
+EARLY = 0
 TABLES = 2
 WAIT = 3
 MESH = pl.DeviceIdType.MESH
@@ -81,7 +81,7 @@
 def kernel(plan, charges, coef, rows, interp, top, root_out, top_out, *scratch):
     (points, mats, picks, nodes, halves, ops, skel, leafw, tops, tables, wide, level_ops, parts,
      below, above, leaving, coming, sums, extra, load_sem, up_send, up_recv, down_send, down_recv,
-     table_send, table_recv, part_send, part_recv, sum_send, sum_recv) = scratch
+     table_send, table_recv, part_send, part_recv, sum_send, sum_recv, hello) = scratch
     R, L, H, Q = plan["R"], plan["L"], plan["H"], plan["Q"]
     leaves, S, M = plan["leaves"], plan["S"], plan["M"]
     m, n_leaf, early = plan["m"], plan["n_leaf"], plan["early"]
@@ -128,15 +128,15 @@
         for k in range(count):
             where[level, k] = len(where)
             copies.append((interp.at[total - (total >> level - 1) + z * count + k], nodes.at[where[level, k]]))
+    soon = len(copies)
     copies.append((top, tops))
-    soon = len(copies)
     loads = [pltpu.make_async_copy(a, b, load_sem.at[chunks + i]) for i, (a, b) in enumerate(copies)]
 
     for copy in loads[:lead]:
         copy.start()
+    chunk_copy(0).start()
     for copy in loads[lead:soon]:
         copy.start()
-    chunk_copy(0).start()
 
     def table_copies(delta):
         peer = flip(p, delta, L)
@@ -154,13 +154,16 @@
 
     def table_stage(k):
         if k > 1:
-            for delta in stages[k - 1]:
-                for copy in table_copies(delta):
-                    copy.wait_recv()
-        if k <= L:
-            for delta in stages[k]:
-                for copy in table_copies(delta):
-                    copy.start()
+            pl.semaphore_wait(hello.at[k - 2], L)
+        else:
+            loads[-1].wait()
+        if k < L:
+            for b in range(L):
+                pl.semaphore_signal(hello.at[k - 1], inc=1, device_id={"leaf": flip(p, 1 << b, L)},
+                                    device_id_type=MESH)
+        for delta in stages[k]:
+            for copy in table_copies(delta):
+                copy.start()
 
     def send_up(i):
         return pltpu.make_async_remote_copy(
@@ -203,13 +206,16 @@
             part = slice(t * 128, (t + 1) * 128)
             mats[n, :, part] = (mats[n, :, part].astype(jnp.float32)
                                 + jnp.where(across == lanes + t * 128, 1.0, 0.0)).astype(bf)
+    for copy in loads[lead:soon]:
+        copy.wait()
+    chunk_copy(0).wait()
+    loads[-1].start()
     for i in range(1, chunks):
         chunk_copy(i).start()
-    for copy in loads[lead:soon]:
-        copy.wait()
 
     def leaf_stage(i):
-        chunk_copy(i).wait()
+        if i > 0:
+            chunk_copy(i).wait()
         for n in range(leaves):
             leafw[n * S:(n + 1) * S, :] = dot(mats[n], points[i, n * M:(n + 1) * M, :]).astype(bf)
 
@@ -248,7 +254,6 @@
             parts[base + j] = value[:, j * PIECE:(j + 1) * PIECE]
         if i == 0:
             pl.semaphore_wait(barrier, neighbours + L)
-            table_stage(1)
         if i < chunks - H and R > 1:
             @pl.when(z == 0)
             def _():
@@ -259,8 +264,13 @@
             def _():
                 for j in range(CHUNK // PIECE):
                     send_down(base + j).start()
+        if i == 0:
+            table_stage(1)
 
     def prepare_top():
+        for delta in range(1, n_leaf):
+            for copy in table_copies(delta):
+                copy.wait_recv()
         for level in range(1, L + 1):
             offset, count = S - (S >> level - 1), S >> level
             half = pl.ds(pl.multiple_of(bit(p, level - 1) * S, S), S)
@@ -448,14 +458,11 @@
         while made < chunks and (made < needed[t] or made < min(t + AHEAD, chunks)):
             chunk(made)
             made += 1
-            if made == AHEAD and stage == 2:
+            if stage <= L and made >= TABLES * (stage - 1):
                 table_stage(stage)
                 stage += 1
-        if made == chunks and stage <= L and t < earliest and t >= TABLES * (stage - 1):
-            table_stage(stage)
-            stage += 1
         if t == earliest:
-            while stage <= L + 1:
+            while stage <= L:
                 table_stage(stage)
                 stage += 1
             prepare_top()
@@ -548,8 +555,8 @@
     dma = pltpu.SemaphoreType.DMA
     results = pl.pallas_call(
         functools.partial(kernel, plan),
-        out_shape=(jax.ShapeDtypeStruct((S, width), bf), jax.ShapeDtypeStruct((pack, width), bf)),
-        in_specs=[any_spec] * 5,
+        out_shape=(pltpu.VMEM((S, width), bf), pltpu.VMEM((pack, width), bf)),
+        in_specs=[pl.BlockSpec(memory_space=pltpu.HBM)] * 5,
         out_specs=(vmem, vmem),
         scratch_shapes=[
             pltpu.VMEM((R * H, leaves * M, CHUNK), bf),
@@ -582,6 +589,7 @@
             dma((Q + EARLY, peers)),
             dma((max(EARLY, 1),)),
             dma((max(EARLY, 1),)),
+            pltpu.SemaphoreType.REGULAR((max(L - 1, 1),)),
         ],
         compiler_params=pltpu.CompilerParams(collective_id=0, has_side_effects=True,
                                              vmem_limit_bytes=60 * 1024 * 1024),
@@ -592,6 +600,7 @@
         in_specs=[vmem, vmem],
         out_specs=(any_spec, any_spec),
         scratch_shapes=[pltpu.SemaphoreType.DMA((2,))],
+        compiler_params=pltpu.CompilerParams(vmem_limit_bytes=4 * 1024 * 1024),
     )(*results)
 
 

time: 35.1 us -> 30.9 us (0.88)
  the two profiles are of different devices: /device:TPU:9 before, /device:TPU:17 now
where the time goes in v3:
time: 30.9 us; the launch traced here: 30.7 us
  Pallas kernels  30.1 us (97%)
  between operations  0.64 us (2%)
    pallas_call x1, Pallas kernels, local(): pl.pallas_call(functools.partial(kernel, plan), out_shape=(pltpu.VMEM((S,...  29.3 us
    pallas_call x1, Pallas kernels, local(): pl.pallas_call(store, out_shape=(jax.ShapeDtypeStruct((S, width), bf), ja...  0.79 us

profile of v3, /device:TPU:17, one launch (start us, length us, event | category | flops | bytes accessed | tf_op | source)
XLA Modules:
  0.0 30.7 jit_solution(4256724967899982777)
XLA Ops:
  0.6 29.3 %shard_map.68 = (bf16[256,512]{1,0:T(8,128)(2,1)S(1)}, bf16[224,512]{1,0:T(8,128)(2,1)S(1)}) custom-call(bf16[2048,2048]{1,0:T(8,128)(2,1)} %charges.1, bf16[4,256,512]{2,1,0:T(8,128)(2,1)} %coef.1, s32[4,256]{1,0:T(4,128)} %rows.1, bf16[15,256,512]{2,1,0:T(8,128)(2,1)} %interp.1, bf16[224,512]{1,0:T(8,128)(2,1)} %top.1), custom_call_target="tpu_custom_call" | custom-call | tf_op jit(solution)/shard_map/pallas_call | solution.py:556
  30.0 0.8 %shard_map.69 = (bf16[256,512]{1,0:T(8,128)(2,1)}, bf16[224,512]{1,0:T(8,128)(2,1)}) custom-call(bf16[256,512]{1,0:T(8,128)(2,1)S(1)} %get-tuple-element.4.root, bf16[224,512]{1,0:T(8,128)(2,1)S(1)} %get-tuple-element.5.top), custom_call_target="tpu_custom_call" | custom-call | tf_op jit(solution)/shard_map/pallas_call | solution.py:597

commit v4 on v3

--- a/solution.py
+++ b/solution.py
@@ -10,7 +10,7 @@
 PIECE = 128
 CHUNK = 256
 LAG = 2
-AHEAD = 5
+AHEAD = 3
 EARLY = 0
 TABLES = 2
 WAIT = 3
@@ -117,7 +117,7 @@
         return pltpu.make_async_copy(
             charges.at[:, pl.ds(pl.multiple_of(column, CHUNK), CHUNK)], points.at[i], load_sem.at[i])
 
-    copies = [(rows, picks)] + [(coef.at[n], mats.at[n]) for n in range(leaves)]
+    copies = [(rows, picks), (coef, mats)]
     lead = len(copies)
     for b in range(m):
         index = total - (total >> early + b) + z // (1 << b + 1)
@@ -125,9 +125,11 @@
     where = {}
     for level in range(early, 0, -1):
         count = leaves >> level
+        base = len(where)
         for k in range(count):
             where[level, k] = len(where)
-            copies.append((interp.at[total - (total >> level - 1) + z * count + k], nodes.at[where[level, k]]))
+        copies.append((interp.at[pl.ds(total - (total >> level - 1) + z * count, count)],
+                       nodes.at[pl.ds(base, count)]))
     soon = len(copies)
     copies.append((top, tops))
     loads = [pltpu.make_async_copy(a, b, load_sem.at[chunks + i]) for i, (a, b) in enumerate(copies)]
@@ -146,9 +148,15 @@
             half = pl.ds(pl.multiple_of(bit(peer, level - 1) * S, S), S)
             out.append(pltpu.make_async_remote_copy(
                 src_ref=tops.at[part, half], dst_ref=tables.at[delta - 1, part],
-                send_sem=table_send.at[delta - 1, level - 1], recv_sem=table_recv.at[delta - 1, level - 1],
+                send_sem=table_send.at[0], recv_sem=table_recv.at[0],
                 device_id={"leaf": peer}, device_id_type=MESH))
         return out
+
+    def all_tables():
+        every = wide.at[pl.ds(0, sum(segs[delta][2] for delta in range(1, n_leaf)))]
+        return pltpu.make_async_remote_copy(
+            src_ref=every, dst_ref=every, send_sem=table_send.at[0], recv_sem=table_recv.at[0],
+            device_id={"leaf": flip(p, 1, L)}, device_id_type=MESH)
 
     stages = [[d for d in range(1, n_leaf) if bin(d).count("1") == k] for k in range(L + 1)]
 
@@ -167,25 +175,38 @@
 
     def send_up(i):
         return pltpu.make_async_remote_copy(
-            src_ref=parts.at[i], dst_ref=below.at[i], send_sem=up_send.at[i], recv_sem=up_recv.at[i],
+            src_ref=parts.at[i], dst_ref=below.at[i], send_sem=up_send.at[i // Q], recv_sem=up_recv.at[i - Q],
             device_id={"rhs": z + 1}, device_id_type=MESH)
 
     def send_down(i):
         return pltpu.make_async_remote_copy(
-            src_ref=parts.at[i], dst_ref=above.at[i], send_sem=down_send.at[i], recv_sem=down_recv.at[i],
+            src_ref=parts.at[i], dst_ref=above.at[i], send_sem=down_send.at[i // Q], recv_sem=down_recv.at[i],
             device_id={"rhs": z - 1}, device_id_type=MESH)
+
+    def whole_block(c, up):
+        ref = pl.ds(c * Q, Q)
+        return pltpu.make_async_remote_copy(
+            src_ref=parts.at[ref], dst_ref=(below if up else above).at[ref],
+            send_sem=(up_send if up else down_send).at[c], recv_sem=(up_recv if up else down_recv).at[0],
+            device_id={"rhs": z + 1 if up else z - 1}, device_id_type=MESH)
 
     def part_copy(q, delta):
         start, _, _, padded = segs[delta]
         ref = pl.ds(start, padded)
         return pltpu.make_async_remote_copy(
-            src_ref=leaving.at[q, ref], dst_ref=coming.at[q, ref], send_sem=part_send.at[q, delta - 1],
-            recv_sem=part_recv.at[q, delta - 1], device_id={"leaf": flip(p, delta, L)}, device_id_type=MESH)
+            src_ref=leaving.at[q, ref], dst_ref=coming.at[q, ref], send_sem=part_send.at[q],
+            recv_sem=part_recv.at[q], device_id={"leaf": flip(p, delta, L)}, device_id_type=MESH)
 
     if hurried:
         @pl.when(chosen(z, [int(k in (1, R - 2)) for k in range(R)]) == 0)
         def _():
             extra[...] = jnp.zeros_like(extra)
+
+    def all_parts(q):
+        ref = pl.ds(segs[1][0], height - segs[1][0])
+        return pltpu.make_async_remote_copy(
+            src_ref=leaving.at[q, ref], dst_ref=coming.at[q, ref], send_sem=part_send.at[q],
+            recv_sem=part_recv.at[q], device_id={"leaf": flip(p, 1, L)}, device_id_type=MESH)
 
     @pl.when(z == 0)
     def _():
@@ -268,9 +289,8 @@
             table_stage(1)
 
     def prepare_top():
-        for delta in range(1, n_leaf):
-            for copy in table_copies(delta):
-                copy.wait_recv()
+        if n_leaf > 1:
+            all_tables().wait_recv()
         for level in range(1, L + 1):
             offset, count = S - (S >> level - 1), S >> level
             half = pl.ds(pl.multiple_of(bit(p, level - 1) * S, S), S)
@@ -322,6 +342,15 @@
                 add_into(s_down, above)
                 send_down(s_down).start()
 
+        finals = [final_step(R, Q, k) for k in range(R)]
+        if any_device(lambda k: 0 <= t - finals[k] < Q):
+            q = t - chosen(z, finals)
+            last = chosen(z, [Q - hurried * late(k) for k in range(R)])
+
+            @pl.when((q >= 0) & (q < last))
+            def _():
+                finish(q)
+
         for j in range(hurried):
             q = Q - hurried + j
             if any_device(lambda k: late(k) and t == hurry_step(k, q)):
@@ -330,15 +359,6 @@
                 @pl.when(now == 1)
                 def _():
                     hurry(q)
-
-        finals = [final_step(R, Q, k) for k in range(R)]
-        if any_device(lambda k: 0 <= t - finals[k] < Q):
-            q = t - chosen(z, finals)
-            last = chosen(z, [Q - hurried * late(k) for k in range(R)])
-
-            @pl.when((q >= 0) & (q < last))
-            def _():
-                finish(q)
 
     def finish(q):
         i = z * Q + q
@@ -357,7 +377,7 @@
 
     def spread(q, value):
         leaving[q] = dot(wide[...], value).astype(bf)
-        for delta in range(1, n_leaf):
+        for delta in sorted(range(1, n_leaf), key=lambda d: (-bin(d >> 1).count("1"), -d)):
             part_copy(q, delta).start()
 
     def late(k):
@@ -365,7 +385,7 @@
 
     def hurry_step(k, q):
         other = LAG * (R - 1 - k) + k * Q if k == 1 else LAG * k + (R - 1 - k) * Q
-        return max((other if R > 2 else 0) + q, earliest)
+        return max((other if R > 2 else 0) + q, final_step(R, Q, k) + Q - hurried - 1)
 
     def hurry(q):
         i = z * Q + q
@@ -390,8 +410,8 @@
             device_id={"rhs": z + 1 if upward else z - 1}, device_id_type=MESH)
 
     def gather(q):
-        for delta in range(1, n_leaf):
-            part_copy(q, delta).wait_recv()
+        if n_leaf > 1:
+            all_parts(q).wait_recv()
         out = []
         for level in range(1, L + 1):
             offset, count = S - (S >> level - 1), S >> level
@@ -472,8 +492,38 @@
             end_finish()
         step(t)
 
+    if n_leaf > 1:
+        all_tables().wait_send()
+    if hurried:
+        @pl.when((z == 0) | (z == R - 1))
+        def _():
+            for j in range(hurried):
+                all_parts(Q + j).wait_send()
+
+        @pl.when(z == 0)
+        def _():
+            for j in range(hurried):
+                sum_copy(j, True).wait_send()
+
+        @pl.when(z == R - 1)
+        def _():
+            for j in range(hurried):
+                sum_copy(j, False).wait_send()
+    if R > 1:
+        for c in range(R):
+            @pl.when((z < R - 1) & (z < c))
+            def _():
+                whole_block(c, True).wait_send()
+
+            @pl.when((z > 0) & (z > c))
+            def _():
+                whole_block(c, False).wait_send()
+
     for q in range(Q):
         j = q - (Q - hurried)
+        if q == Q - 1 and n_leaf > 1:
+            for k in range(Q - 1):
+                all_parts(k).wait_send()
         columns = slice(q * PIECE, (q + 1) * PIECE)
         values = gather(q)
         if j >= 0:
@@ -495,36 +545,8 @@
                 value = value + extra[j, offset:offset + count, :].astype(jnp.float32)
             top_out[offset:offset + count, columns] = value.astype(bf)
 
-    for delta in range(1, n_leaf):
-        for copy in table_copies(delta):
-            copy.wait_send()
-        for q in range(Q):
-            part_copy(q, delta).wait_send()
-    if hurried:
-        @pl.when((z == 0) | (z == R - 1))
-        def _():
-            for j in range(hurried):
-                for delta in range(1, n_leaf):
-                    part_copy(Q + j, delta).wait_send()
-
-        @pl.when(z == 0)
-        def _():
-            for j in range(hurried):
-                sum_copy(j, True).wait_send()
-
-        @pl.when(z == R - 1)
-        def _():
-            for j in range(hurried):
-                sum_copy(j, False).wait_send()
-    if R > 1:
-        for i in range(R * Q):
-            @pl.when((z < R - 1) & (z < i // Q))
-            def _():
-                send_up(i).wait_send()
-
-            @pl.when((z > 0) & (z > i // Q))
-            def _():
-                send_down(i).wait_send()
+    if n_leaf > 1:
+        all_parts(Q - 1).wait_send()
 
 
 def store(root, top, root_out, top_out, sems):
@@ -578,15 +600,15 @@
             pltpu.VMEM((Q + EARLY, height, PIECE), bf),
             pltpu.VMEM((max(EARLY, 1), pack, PIECE), bf),
             pltpu.VMEM((max(EARLY, 1), pack, PIECE), bf),
-            dma((R * H + 2 + leaves + node_count + m,)),
-            dma((R * Q,)),
-            dma((R * Q,)),
-            dma((R * Q,)),
-            dma((R * Q,)),
-            dma((peers, max(L, 1))),
-            dma((peers, max(L, 1))),
-            dma((Q + EARLY, peers)),
-            dma((Q + EARLY, peers)),
+            dma((R * H + 3 + early + m,)),
+            dma((R,)),
+            dma((max(R - 1, 1) * Q,)),
+            dma((R,)),
+            dma((max(R - 1, 1) * Q,)),
+            dma((1,)),
+            dma((1,)),
+            dma((Q + EARLY,)),
+            dma((Q + EARLY,)),
             dma((max(EARLY, 1),)),
             dma((max(EARLY, 1),)),
             pltpu.SemaphoreType.REGULAR((max(L - 1, 1),)),

time: 30.9 us -> 29 us (0.939)
  Pallas kernels: 30.1 us -> 28.1 us
    pallas_call x1, Pallas kernels: 29.3 us -> 27.3 us  [local(): pl.pallas_call(functools.partial(kernel, plan), out_shape=(pltpu.VMEM((S,...]
where the time goes in v4:
time: 29 us; the launch traced here: 28.7 us
  Pallas kernels  28.1 us (97%)
  between operations  0.64 us (2%)
    pallas_call x1, Pallas kernels, local(): pl.pallas_call(functools.partial(kernel, plan), out_shape=(pltpu.VMEM((S,...  27.3 us
    pallas_call x1, Pallas kernels, local(): pl.pallas_call(store, out_shape=(jax.ShapeDtypeStruct((S, width), bf), ja...  0.79 us

profile of v4, /device:TPU:17, one launch (start us, length us, event | category | flops | bytes accessed | tf_op | source)
XLA Modules:
  0.0 28.7 jit_solution(3914884366459403065)
XLA Ops:
  0.6 27.3 %shard_map.68 = (bf16[256,512]{1,0:T(8,128)(2,1)S(1)}, bf16[224,512]{1,0:T(8,128)(2,1)S(1)}) custom-call(bf16[2048,2048]{1,0:T(8,128)(2,1)} %charges.1, bf16[4,256,512]{2,1,0:T(8,128)(2,1)} %coef.1, s32[4,256]{1,0:T(4,128)} %rows.1, bf16[15,256,512]{2,1,0:T(8,128)(2,1)} %interp.1, bf16[224,512]{1,0:T(8,128)(2,1)} %top.1), custom_call_target="tpu_custom_call" | custom-call | tf_op jit(solution)/shard_map/pallas_call | solution.py:578
  27.9 0.8 %shard_map.69 = (bf16[256,512]{1,0:T(8,128)(2,1)}, bf16[224,512]{1,0:T(8,128)(2,1)}) custom-call(bf16[256,512]{1,0:T(8,128)(2,1)S(1)} %get-tuple-element.4.root, bf16[224,512]{1,0:T(8,128)(2,1)S(1)} %get-tuple-element.5.top), custom_call_target="tpu_custom_call" | custom-call | tf_op jit(solution)/shard_map/pallas_call | solution.py:619

commit v5 on v4

--- a/solution.py
+++ b/solution.py
@@ -136,9 +136,9 @@
 
     for copy in loads[:lead]:
         copy.start()
-    chunk_copy(0).start()
     for copy in loads[lead:soon]:
         copy.start()
+    chunk_copy(0).start()
 
     def table_copies(delta):
         peer = flip(p, delta, L)
@@ -217,22 +217,6 @@
     def _():
         for q in range(Q):
             above[(R - 1) * Q + q] = jnp.zeros((S, PIECE), bf)
-
-    for copy in loads[:lead]:
-        copy.wait()
-    lanes = lax.broadcasted_iota(jnp.int32, (S, 128), 1)
-    for n in range(leaves):
-        across = jnp.transpose(jnp.broadcast_to(picks[n:n + 1, :], (128, S)))
-        for t in range(M // 128):
-            part = slice(t * 128, (t + 1) * 128)
-            mats[n, :, part] = (mats[n, :, part].astype(jnp.float32)
-                                + jnp.where(across == lanes + t * 128, 1.0, 0.0)).astype(bf)
-    for copy in loads[lead:soon]:
-        copy.wait()
-    chunk_copy(0).wait()
-    loads[-1].start()
-    for i in range(1, chunks):
-        chunk_copy(i).start()
 
     def leaf_stage(i):
         if i > 0:
@@ -266,8 +250,6 @@
 
     def chunk(i):
         leaf_stage(i)
-        if i == 0:
-            compose()
         value = dot(skel[...], leafw[...]).astype(bf)
         c = block(i // H)
         base = c * Q + i % H * (CHUNK // PIECE)
@@ -376,8 +358,11 @@
         spread(q, root)
 
     def spread(q, value):
-        leaving[q] = dot(wide[...], value).astype(bf)
+        cut = segs[2][0] if n_leaf > 2 else 0
+        leaving[q, cut:, :] = dot(wide[cut:, :], value).astype(bf)
         for delta in sorted(range(1, n_leaf), key=lambda d: (-bin(d >> 1).count("1"), -d)):
+            if delta == 1 and cut:
+                leaving[q, :cut, :] = dot(wide[:cut, :], value).astype(bf)
             part_copy(q, delta).start()
 
     def late(k):
@@ -472,6 +457,21 @@
         if t >= earliest:
             need = max(need, chunks if hurried else 0)
         needed.append(need)
+
+    for copy in loads[:soon]:
+        copy.wait()
+    lanes = lax.broadcasted_iota(jnp.int32, (S, 128), 1)
+    for n in range(leaves):
+        across = jnp.transpose(jnp.broadcast_to(picks[n:n + 1, :], (128, S)))
+        for t in range(M // 128):
+            part = slice(t * 128, (t + 1) * 128)
+            mats[n, :, part] = (mats[n, :, part].astype(jnp.float32)
+                                + jnp.where(across == lanes + t * 128, 1.0, 0.0)).astype(bf)
+    compose()
+    chunk_copy(0).wait()
+    loads[-1].start()
+    for i in range(1, chunks):
+        chunk_copy(i).start()
 
     made, stage = 0, 2
     for t in range(steps):

time: 29 us -> 29 us (level)
  no operation moved by 1% of the time
where the time goes in v5:
time: 29 us; the launch traced here: 28.7 us
  Pallas kernels  28.1 us (97%)
  between operations  0.64 us (2%)
    pallas_call x1, Pallas kernels, local(): pl.pallas_call(functools.partial(kernel, plan), out_shape=(pltpu.VMEM((S,...  27.3 us
    pallas_call x1, Pallas kernels, local(): pl.pallas_call(store, out_shape=(jax.ShapeDtypeStruct((S, width), bf), ja...  0.79 us

profile of v5, /device:TPU:17, one launch (start us, length us, event | category | flops | bytes accessed | tf_op | source)
XLA Modules:
  0.0 28.7 jit_solution(10415734433211563649)
XLA Ops:
  0.6 27.3 %shard_map.68 = (bf16[256,512]{1,0:T(8,128)(2,1)S(1)}, bf16[224,512]{1,0:T(8,128)(2,1)S(1)}) custom-call(bf16[2048,2048]{1,0:T(8,128)(2,1)} %charges.1, bf16[4,256,512]{2,1,0:T(8,128)(2,1)} %coef.1, s32[4,256]{1,0:T(4,128)} %rows.1, bf16[15,256,512]{2,1,0:T(8,128)(2,1)} %interp.1, bf16[224,512]{1,0:T(8,128)(2,1)} %top.1), custom_call_target="tpu_custom_call" | custom-call | tf_op jit(solution)/shard_map/pallas_call | solution.py:578
  27.9 0.8 %shard_map.69 = (bf16[256,512]{1,0:T(8,128)(2,1)}, bf16[224,512]{1,0:T(8,128)(2,1)}) custom-call(bf16[256,512]{1,0:T(8,128)(2,1)S(1)} %get-tuple-element.4.root, bf16[224,512]{1,0:T(8,128)(2,1)S(1)} %get-tuple-element.5.top), custom_call_target="tpu_custom_call" | custom-call | tf_op jit(solution)/shard_map/pallas_call | solution.py:619
